TPU v7x, 32 devices: a whole 2x2x4 slice. The times are simulated.
32 devices in a mesh: ma: 16 (over z, x, core), dev: 2 (over y).
Axes of the slice: x: 2, y: 2, z: 4, core: 2. Of those that a mesh axis runs over, the one named last changes fastest.
Arguments:
- grid_latent: bfloat16 [16384, 512], P('ma'), may hold values from -6 to 6
- mesh_latent: bfloat16 [10240, 512], P('ma'), may hold values from -6 to 6
- grid_map: int32 [10240, 4], P('ma'), may hold values from 0 to 16383, as said below
- fine_senders: int32 [10240, 6], P('ma'), may hold values from 0 to 10239, as said below
- coarse_senders: int32 [256, 24], P('ma'), may hold values from 0 to 255
- fine_geom: float32 [10240, 6, 4], P('ma'), may hold values from -6 to 6
- coarse_geom: float32 [256, 24, 4], P('ma'), may hold values from -6 to 6
- w_send: bfloat16 [2, 512, 512], P(None, None, 'dev'), may hold values from -0.1875 to 0.1875
- w_recv: bfloat16 [2, 512, 512], P(None, None, 'dev'), may hold values from -0.1875 to 0.1875
- w_geom: float32 [2, 4, 512], P(None, None, 'dev'), may hold values from -2 to 2
- edge_bias: float32 [2, 512], P(None, 'dev'), may hold values from -3 to 3
- w_msg: bfloat16 [2, 512, 512], P(None, 'dev'), may hold values from -0.25 to 0.25
- msg_bias: float32 [2, 512], replicated, may hold values from -2 to 2
- w_node_h: bfloat16 [2, 512, 512], P(None, None, 'dev'), may hold values from -0.1875 to 0.1875
- w_node_a: bfloat16 [2, 512, 512], P(None, None, 'dev'), may hold values from -0.125 to 0.125
- node_bias: float32 [2, 512], P(None, 'dev'), may hold values from -3 to 3
- w_node_out: bfloat16 [2, 512, 512], P(None, 'dev'), may hold values from -0.25 to 0.25
- norm_gain: float32 [2, 512], replicated, may hold values from 0.25 to 1.75
- norm_bias: float32 [2, 512], replicated, may hold values from -2 to 2
Outputs:
- new_latent: bfloat16 [10240, 512], P('ma')
Inputs may be any that keep to these rules, and one draw needn't show every extreme that they name: For a node n in patch p = n // 640, every grid_map[n, k] equals (p * 1024 + o) modulo 16384 with -512 <= o < 1536; both ends of that band are used in every patch. For a node n in patch p = n // 640, every fine_senders[n, j] equals (p * 640 + o) modulo 10240 with -320 <= o < 960; both ends of that band are used in every patch. `coarse_senders`: any coarse node may send to any coarse node.
All inputs are finite; a program needn't handle non-finite values.
Results may differ from a plain program's by a relative error of at most 0.015.
Values may be sent and summed in bfloat16 or wider, within the bound.
A program may use at most 64 MiB of HBM per device.

v0:
```python
import jax
import jax.numpy as jnp
from jax import lax
from jax.sharding import PartitionSpec as P

norm_eps = 1e-05


def padded_2(block, sides, width, periodic):
    for axis, dim in sides:
        count = lax.axis_size(axis)
        forward = [(i, i + 1) for i in range(count - 1)]
        if periodic:
            forward.append((count - 1, 0))
        backward = [(target, source) for source, target in forward]
        low = lax.ppermute(
            lax.slice_in_dim(block, block.shape[dim] - width, None, axis=dim), axis, forward
        )
        high = lax.ppermute(lax.slice_in_dim(block, 0, width, axis=dim), axis, backward)
        block = jnp.concatenate([low, block, high], axis=dim)
    return block


def edge_messages(send_rows, recv_rows, geom, geom_weight, bias_edge, msg_weight):
    count, fan_in = (send_rows.shape[0], send_rows.shape[1])
    geom_term = jnp.einsum("nkg,gd->nkd", geom, geom_weight, precision=lax.Precision.HIGHEST)
    preact = (
        send_rows.astype(jnp.float32)
        + recv_rows[:, None, :].astype(jnp.float32)
        + geom_term
        + bias_edge
    )
    hidden = jax.nn.silu(preact).astype(jnp.bfloat16).reshape(count * fan_in, send_rows.shape[2])
    product = jnp.dot(hidden, msg_weight, preferred_element_type=jnp.float32)
    return jnp.sum(product.reshape(count, fan_in, msg_weight.shape[1]), axis=1)


def node_layer(latent, agg, weight_h, weight_a, bias_node):
    node_pre = (
        jnp.dot(latent, weight_h, preferred_element_type=jnp.float32)
        + jnp.dot(agg, weight_a, preferred_element_type=jnp.float32)
        + bias_node
    )
    return jax.nn.silu(node_pre).astype(jnp.bfloat16)


def per_device(
    grid_latent,
    mesh_latent,
    grid_map,
    fine_senders,
    coarse_senders,
    fine_geom,
    coarse_geom,
    w_send,
    w_recv,
    w_geom,
    edge_bias,
    w_msg,
    msg_bias,
    w_node_h,
    w_node_a,
    node_bias,
    w_node_out,
    norm_gain,
    norm_bias,
):
    node_dev, features = mesh_latent.shape
    grid_dev = grid_latent.shape[0]
    patches = lax.axis_size("ma")
    patch_id = lax.axis_index("ma")
    dev_id = lax.axis_index("dev")
    co_dev, coarse_in = coarse_senders.shape
    fine_in = fine_senders.shape[1]
    grid_border = grid_dev // 2
    node_border = node_dev // 2
    padded_grid = padded_2(grid_latent, (("ma", 0),), grid_border, True)
    local_map = (grid_map - patch_id * grid_dev + grid_border) % (grid_dev * patches)
    pulled = jnp.take(padded_grid, local_map, axis=0).astype(jnp.float32)
    latent = (mesh_latent.astype(jnp.float32) + jnp.mean(pulled, axis=1)).astype(jnp.bfloat16)
    local_senders = (fine_senders - patch_id * node_dev + node_border) % (node_dev * patches)
    own = node_dev // lax.axis_size("dev")
    first = dev_id * own
    full_send, full_recv, full_h, full_a = (
        lax.all_gather(w_send, "dev", axis=2, tiled=True),
        lax.all_gather(w_recv, "dev", axis=2, tiled=True),
        lax.all_gather(w_node_h, "dev", axis=2, tiled=True),
        lax.all_gather(w_node_a, "dev", axis=2, tiled=True),
    )
    full_msg, full_out = (
        lax.all_gather(w_msg, "dev", axis=1, tiled=True),
        lax.all_gather(w_node_out, "dev", axis=1, tiled=True),
    )
    full_geom, full_ebias, full_nbias = (
        lax.all_gather(w_geom, "dev", axis=2, tiled=True),
        lax.all_gather(edge_bias[:, None, :], "dev", axis=2, tiled=True),
        lax.all_gather(node_bias[:, None, :], "dev", axis=2, tiled=True),
    )
    latent = lax.dynamic_slice_in_dim(latent, first, own, 0)
    senders_own = lax.dynamic_slice_in_dim(local_senders, first, own, 0)
    geom_own = lax.dynamic_slice_in_dim(fine_geom, first, own, 0)
    keep_coarse = (dev_id == 0).astype(jnp.float32)
    position = first + jnp.arange(own, dtype=jnp.int32)
    is_coarse_own = (position < co_dev).astype(jnp.float32)
    counts_own = (fine_in + coarse_in * is_coarse_own)[:, None]
    for pass_idx in range(w_send.shape[0]):
        send_half = jnp.dot(latent, full_send[pass_idx], preferred_element_type=jnp.float32).astype(
            jnp.bfloat16
        )
        recv_half = jnp.dot(latent, full_recv[pass_idx], preferred_element_type=jnp.float32).astype(
            jnp.bfloat16
        )
        geom_weight = full_geom[pass_idx]
        bias_edge = full_ebias[pass_idx][0]
        msg_weight = full_msg[pass_idx]
        send_patch = lax.all_gather(send_half, "dev", axis=0, tiled=True)
        padded = padded_2(send_patch, (("ma", 0),), node_border, True)
        fine_sum = edge_messages(
            padded[senders_own], recv_half, geom_own, geom_weight, bias_edge, msg_weight
        )
        everyone = lax.all_gather(send_patch[:co_dev], "ma", axis=0, tiled=True)
        coarse_sum = (
            edge_messages(
                everyone[coarse_senders],
                recv_half[:co_dev],
                coarse_geom,
                geom_weight,
                bias_edge,
                msg_weight,
            )
            * keep_coarse
        )
        partial_value = jnp.concatenate([fine_sum[:co_dev] + coarse_sum, fine_sum[co_dev:]], axis=0)
        agg = (partial_value + counts_own * msg_bias[pass_idx][None, :]).astype(jnp.bfloat16)
        node_hidden = node_layer(
            latent, agg, full_h[pass_idx], full_a[pass_idx], full_nbias[pass_idx][0]
        )
        update = jnp.dot(node_hidden, full_out[pass_idx], preferred_element_type=jnp.float32)
        average = jnp.mean(update, axis=1, keepdims=True)
        spread = jnp.mean(update * update, axis=1, keepdims=True) - average * average
        normed = (update - average) * lax.rsqrt(spread + norm_eps) * norm_gain[
            pass_idx
        ] + norm_bias[pass_idx]
        latent = (latent.astype(jnp.float32) + normed).astype(jnp.bfloat16)
    latent = lax.all_gather(latent, "dev", axis=0, tiled=True)
    return latent


def solution(mesh):
    in_specs = (
        P("ma", None),
        P("ma", None),
        P("ma", None),
        P("ma", None),
        P("ma", None),
        P("ma", None, None),
        P("ma", None, None),
        P(None, None, "dev"),
        P(None, None, "dev"),
        P(None, None, "dev"),
        P(None, "dev"),
        P(None, "dev", None),
        P(),
        P(None, None, "dev"),
        P(None, None, "dev"),
        P(None, "dev"),
        P(None, "dev", None),
        P(),
        P(),
    )
    out_specs = P("ma", None)
    return jax.shard_map(
        per_device, mesh=mesh, in_specs=in_specs, out_specs=out_specs, check_vma=False
    )
```

profile of v0, /device:TPU:1, one launch (start us, length us, event | category | flops | bytes accessed | tf_op | source)
XLA Modules:
  0.0 233.6 jit_solution(2524247931686585568)
XLA Ops:
  10.1 2.6 %collective-permute-start = (bf16[512,512]{1,0:T(8,128)(2,1)S(1)}, bf16[512,512]{1,0:T(8,128)(2,1)S(1)}, u32[]{:S(2)}, u32[]{:S(2)}) collective-permute-start(bf16[512,512]{1,0:T(8,128)(2,1)S(1)} %get-tuple-element.11), channel_id=1, source_target_pairs={{0,2},{2,4},{4,6},{6,8},{8,10},{10,12},{12,14},{14,16},{16,18},{18... | collective-permute-start | bytes 1572872 | tf_op jit(solution)/shard_map/ppermute | solution.py:16
  13.9 3.5 %all_gather.46 = f32[2,4,512]{2,1,0:T(4,128)S(1)} all-gather(f32[2,4,256]{2,1,0:T(4,128)S(1)} %copy-done.15), channel_id=1, replica_groups=mesh['ma'=16,'dev'=2] {'dev'}, dimensions={2}, use_global_device_ids=true | all-gather | bytes 24576 | tf_op jit(solution)/shard_map/all_gather | solution.py:95
  17.4 3.5 %all-gather = f32[2,512]{1,0:T(2,128)S(1)} all-gather(f32[2,256]{1,0:T(2,128)S(1)} %copy-done.21), channel_id=2, replica_groups=mesh['ma'=16,'dev'=2] {'dev'}, dimensions={1}, use_global_device_ids=true | all-gather | bytes 6144 | tf_op jit(solution)/shard_map/all_gather | solution.py:96
  21.0 3.9 %all-gather.1 = f32[2,512]{1,0:T(2,128)S(1)} all-gather(f32[2,256]{1,0:T(2,128)S(1)} %copy-done.22), channel_id=3, replica_groups=mesh['ma'=16,'dev'=2] {'dev'}, dimensions={1}, use_global_device_ids=true | all-gather | bytes 6144 | tf_op jit(solution)/shard_map/all_gather | solution.py:97
  28.7 8.2 %gather_fusion = bf16[2560,512]{1,0:T(8,128)(2,1)} fusion(bf16[2048,512]{1,0:T(8,128)(2,1)S(1)} %pad_maximum_fusion, s32[3072]{0:T(1024)S(1)} %pad_clamp_fusion), kind=kCustom, calls=%fused_computation | custom fusion | bytes 5253120 | tf_op jit(solution)/shard_map/jit(_take)/gather | solution.py:79
  36.9 3.5 %reshape.75 = bf16[640,4,512]{2,1,0:T(4,128)(2,1)S(1)} reshape(bf16[2560,512]{1,0:T(8,128)(2,1)} %gather_fusion) | data formatting | bytes 5242880 | tf_op jit(solution)/shard_map/jit(_take)/gather | solution.py:79
  40.5 13.7 %convert_reduce_fusion = f32[640,512]{1,0:T(8,128)S(1)} fusion(bf16[640,4,512]{2,1,0:T(4,128)(2,1)S(1)} %reshape.75, pred[640,4]{1,0:T(8,128)(4,1)S(1)} %copy.26), kind=kLoop, calls=%fused_computation.5 | loop fusion | flops 3604480 | bytes 3934720 | tf_op jit(solution)/shard_map/reduce_sum | solution.py:80
  55.8 6.6 %all_gather.44 = bf16[640,512]{1,0:T(8,128)(2,1)S(1)} all-gather(bf16[320,512]{1,0:T(8,128)(2,1)S(1)} %convolution_convert_fusion.3), channel_id=1, replica_groups=mesh['ma'=16,'dev'=2] {'dev'}, dimensions={0}, use_global_device_ids=true | all-gather | bytes 983040 | tf_op jit(solution)/shard_map/all_gather | solution.py:116
  62.5 4.0 %collective-permute-start.2 = (bf16[320,512]{1,0:T(8,128)(2,1)S(1)}, bf16[320,512]{1,0:T(8,128)(2,1)S(1)}, u32[]{:S(2)}, u32[]{:S(2)}) collective-permute-start(bf16[320,512]{1,0:T(8,128)(2,1)S(1)} %get-tuple-element.15), channel_id=1, source_target_pairs={{0,2},{2,4},{4,6},{6,8},{8,10},{10,12},{12,14},{14,16},{16,18},{18... | collective-permute-start | bytes 983048 | tf_op jit(solution)/shard_map/ppermute | solution.py:16
  66.5 4.9 %collective-permute-start.3 = (bf16[320,512]{1,0:T(8,128)(2,1)S(1)}, bf16[320,512]{1,0:T(8,128)(2,1)}, u32[]{:S(2)}, u32[]{:S(2)}) collective-permute-start(bf16[320,512]{1,0:T(8,128)(2,1)S(1)} %get-tuple-element.16), channel_id=1, source_target_pairs={{2,0},{4,2},{6,4},{8,6},{10,8},{12,10},{14,12},{16,14},{18,16},{20... | collective-permute-start | bytes 983048 | tf_op jit(solution)/shard_map/ppermute | solution.py:19
  71.4 25.7 %all_gather.49 = bf16[256,512]{1,0:T(8,128)(2,1)S(1)} all-gather(bf16[16,512]{1,0:T(8,128)(2,1)S(1)} %slice.175), channel_id=1, replica_groups=mesh['ma'=16,'dev'=2] {'ma'}, dimensions={0}, use_global_device_ids=true | all-gather | bytes 278528 | tf_op jit(solution)/shard_map/all_gather | solution.py:121
  97.1 2.2 fusion.55
  107.2 6.4 %gather_fusion.1 = bf16[1920,512]{1,0:T(8,128)(2,1)S(1)} fusion(bf16[1280,512]{1,0:T(8,128)(2,1)S(1)} %pad_maximum_fusion.1, s32[2048]{0:T(1024)S(1)} %pad_clamp_fusion.1), kind=kCustom, calls=%fused_computation.1 | custom fusion | bytes 3939840 | tf_op jit(solution)/shard_map/gather | solution.py:119
  113.7 2.9 %reshape.134 = f32[320,6,512]{2,1,0:T(8,128)} reshape(bf16[1920,512]{1,0:T(8,128)(2,1)S(1)} %gather_fusion.1) | data formatting | bytes 5898240 | tf_op jit(solution)/shard_map/convert_element_type | solution.py:28
  116.5 7.5 %multiply_convert_fusion.1 = bf16[320,6,512]{2,0,1:T(8,128)(2,1)S(1)} fusion(f32[320,6,512]{2,1,0:T(8,128)} %reshape.134, f32[512]{0:T(512)S(1)} %bitcast.103, f32[320,512]{1,0:T(8,128)S(1)} %copy-done.9, f32[640,6,4]{0,2,1:T(4,128)S(1)} %copy-done, s32[]{:T(128)S(6)} %select_n.38, f32[2,4,512]{2,1,0:T(4,128)S(1)} %all_gather.46), kind=kOutput, calls=%fused_computation.13 | convolution fusion | flops 55050240 | bytes 6600708 | tf_op jit(solution)/shard_map/nkg,gd->nkd/dot_general | solution.py:26
  125.3 20.1 %all-gather.19.cloned.1.call-done = bf16[2,512,512]{2,1,0:T(8,128)(2,1)} async-done(((bf16[2,256,512]{2,1,0:T(8,128)(2,1)}), bf16[2,512,512]{2,1,0:T(8,128)(2,1)}) %all-gather.19.cloned.1.call-update) | async-done | bytes 1048592 | tf_op jit(solution)/shard_map/all_gather | solution.py:92
  149.3 9.0 %all_gather.53 = bf16[640,512]{1,0:T(8,128)(2,1)S(1)} all-gather(bf16[320,512]{1,0:T(8,128)(2,1)S(1)} %convolution_convert_fusion.1), channel_id=1, replica_groups=mesh['ma'=16,'dev'=2] {'dev'}, dimensions={0}, use_global_device_ids=true | all-gather | bytes 983040 | tf_op jit(solution)/shard_map/all_gather | solution.py:116
  158.4 23.8 %all_gather.54 = bf16[256,512]{1,0:T(8,128)(2,1)S(1)} all-gather(bf16[16,512]{1,0:T(8,128)(2,1)S(1)} %slice.190), channel_id=1, replica_groups=mesh['ma'=16,'dev'=2] {'ma'}, dimensions={0}, use_global_device_ids=true | all-gather | bytes 278528 | tf_op jit(solution)/shard_map/all_gather | solution.py:121
  188.6 4.4 %collective-permute-done.4 = bf16[320,512]{1,0:T(8,128)(2,1)S(1)} collective-permute-done((bf16[320,512]{1,0:T(8,128)(2,1)S(1)}, bf16[320,512]{1,0:T(8,128)(2,1)S(1)}, u32[]{:S(2)}, u32[]{:S(2)}) %collective-permute-start.4) | collective-permute-done | bytes 327712 | tf_op jit(solution)/shard_map/ppermute | solution.py:16
  193.0 2.8 %collective-permute-done.5 = bf16[320,512]{1,0:T(8,128)(2,1)S(1)} collective-permute-done((bf16[320,512]{1,0:T(8,128)(2,1)S(1)}, bf16[320,512]{1,0:T(8,128)(2,1)S(1)}, u32[]{:S(2)}, u32[]{:S(2)}) %collective-permute-start.5) | collective-permute-done | bytes 327712 | tf_op jit(solution)/shard_map/ppermute | solution.py:19
  195.8 6.4 %gather_fusion.3 = bf16[1920,512]{1,0:T(8,128)(2,1)S(1)} fusion(bf16[1280,512]{1,0:T(8,128)(2,1)S(1)} %pad_maximum_fusion.2, s32[2048]{0:T(1024)S(1)} %pad_clamp_fusion.1), kind=kCustom, calls=%fused_computation.3 | custom fusion | bytes 3939840 | tf_op jit(solution)/shard_map/gather | solution.py:119
  202.2 2.9 %reshape.136 = f32[320,6,512]{2,1,0:T(8,128)} reshape(bf16[1920,512]{1,0:T(8,128)(2,1)S(1)} %gather_fusion.3) | data formatting | bytes 5898240 | tf_op jit(solution)/shard_map/convert_element_type | solution.py:28
  205.1 7.5 %multiply_convert_fusion = bf16[320,6,512]{2,0,1:T(8,128)(2,1)S(1)} fusion(f32[320,6,512]{2,1,0:T(8,128)} %reshape.136, f32[512]{0:T(512)S(1)} %bitcast.99, f32[320,512]{1,0:T(8,128)S(1)} %copy-done.8, f32[640,6,4]{0,2,1:T(4,128)S(1)} %copy-done, s32[]{:T(128)S(6)} %select_n.38, f32[2,4,512]{2,1,0:T(4,128)S(1)} %all_gather.46), kind=kOutput, calls=%fused_computation.12 | convolution fusion | flops 55050240 | bytes 6600708 | tf_op jit(solution)/shard_map/nkg,gd->nkd/dot_general | solution.py:26
  216.2 9.7 %all_gather.55 = bf16[640,512]{1,0:T(8,128)(2,1)S(1)} all-gather(bf16[320,512]{1,0:T(8,128)(2,1)S(1)} %add_convert_fusion), channel_id=1, replica_groups=mesh['ma'=16,'dev'=2] {'dev'}, dimensions={0}, use_global_device_ids=true | all-gather | bytes 983040 | tf_op jit(solution)/shard_map/all_gather | solution.py:145
  (133 shorter events, 33.8 us)
Async XLA Ops:
  6.5 110.0 %copy-start = (f32[640,6,4]{0,2,1:T(4,128)S(1)}, f32[640,6,4]{0,2,1:T(4,128)}, u32[]{:S(2)}) copy-start(f32[640,6,4]{0,2,1:T(4,128)} %param.24) | copy-start | bytes 184324
  6.5 47.8 %all-gather.11.cloned.1.call-start = ((), (), s32[]{:S(2)}) async-start(), calls=%async_computation.1 | async-start | bytes 1572864 | tf_op jit(solution)/shard_map/all_gather | solution.py:85
  7.3 89.9 %all-gather.13.cloned.1.call-start = ((), (), s32[]{:S(2)}) async-start(), calls=%async_computation.2 | async-start | bytes 1572864 | tf_op jit(solution)/shard_map/all_gather | solution.py:86
  8.0 9.4 %copy-start.21 = (f32[2,256]{1,0:T(2,128)S(1)}, f32[2,256]{1,0:T(2,128)}, u32[]{:S(2)}) copy-start(f32[2,256]{1,0:T(2,128)} %param.29) | copy-start | bytes 6148
  8.0 12.9 %copy-start.16 = (s32[16,24]{1,0:T(8,128)S(1)}, s32[16,24]{1,0:T(8,128)}, u32[]{:S(2)}) copy-start(s32[16,24]{1,0:T(8,128)} %param.23) | copy-start | bytes 4612
  8.1 13.0 %copy-start.22 = (f32[2,256]{1,0:T(2,128)S(1)}, f32[2,256]{1,0:T(2,128)}, u32[]{:S(2)}) copy-start(f32[2,256]{1,0:T(2,128)} %param.34) | copy-start | bytes 6148
  8.1 94.4 %all-gather.15.cloned.1.call-start = ((), (), s32[]{:S(2)}) async-start(), calls=%async_computation.3 | async-start | bytes 1572864 | tf_op jit(solution)/shard_map/all_gather | solution.py:91
  8.8 16.1 %copy-start.18 = (f32[2,512]{1,0:T(2,128)S(1)}, f32[2,512]{1,0:T(2,128)}, u32[]{:S(2)}) copy-start(f32[2,512]{1,0:T(2,128)} %param.31) | copy-start | bytes 12292
  8.8 16.2 %copy-start.19 = (f32[2,512]{1,0:T(2,128)S(1)}, f32[2,512]{1,0:T(2,128)}, u32[]{:S(2)}) copy-start(f32[2,512]{1,0:T(2,128)} %param.36) | copy-start | bytes 12292
  8.8 16.2 %copy-start.20 = (f32[2,512]{1,0:T(2,128)S(1)}, f32[2,512]{1,0:T(2,128)}, u32[]{:S(2)}) copy-start(f32[2,512]{1,0:T(2,128)} %param.37) | copy-start | bytes 12292
  8.8 95.1 %all-gather.9.cloned.1.call-start = ((), (), s32[]{:S(2)}) async-start(), calls=%async_computation | async-start | bytes 1572864 | tf_op jit(solution)/shard_map/all_gather | solution.py:87
  9.4 115.9 %all-gather.17.cloned.1.call-start = ((), (), s32[]{:S(2)}) async-start(), calls=%async_computation.4 | async-start | bytes 1572864 | tf_op jit(solution)/shard_map/all_gather | solution.py:88
  10.0 135.5 %all-gather.19.cloned.1.call-start = ((), (), s32[]{:S(2)}) async-start(), calls=%async_computation.5 | async-start | bytes 1572864 | tf_op jit(solution)/shard_map/all_gather | solution.py:92
  10.1 14.9 %collective-permute-start = (bf16[512,512]{1,0:T(8,128)(2,1)S(1)}, bf16[512,512]{1,0:T(8,128)(2,1)S(1)}, u32[]{:S(2)}, u32[]{:S(2)}) collective-permute-start(bf16[512,512]{1,0:T(8,128)(2,1)S(1)} %get-tuple-element.11), channel_id=1, source_target_pairs={{0,2},{2,4},{4,6},{6,8},{8,10},{10,12},{12,14},{14,16},{16,18},{18... | collective-permute-start | bytes 1572872 | tf_op jit(solution)/shard_map/ppermute | solution.py:16
  12.8 14.6 %collective-permute-start.1 = (bf16[512,512]{1,0:T(8,128)(2,1)S(1)}, bf16[512,512]{1,0:T(8,128)(2,1)}, u32[]{:S(2)}, u32[]{:S(2)}) collective-permute-start(bf16[512,512]{1,0:T(8,128)(2,1)S(1)} %get-tuple-element.12), channel_id=1, source_target_pairs={{2,0},{4,2},{6,4},{8,6},{10,8},{12,10},{14,12},{16,14},{18,16},{20... | collective-permute-start | bytes 1572872 | tf_op jit(solution)/shard_map/ppermute | solution.py:19
  40.5 13.7 %copy-start.13 = (bf16[640,512]{1,0:T(8,128)(2,1)S(1)}, bf16[640,512]{1,0:T(8,128)(2,1)}, u32[]{:S(2)}) copy-start(bf16[640,512]{1,0:T(8,128)(2,1)} %param.20) | copy-start | bytes 1966084
  54.3 49.6 %copy-start.3 = (bf16[320,512]{1,0:T(8,128)(2,1)}, bf16[320,512]{1,0:T(8,128)(2,1)S(1)}, u32[]{:S(2)}) copy-start(bf16[320,512]{1,0:T(8,128)(2,1)S(1)} %fusion.9) | copy-start | bytes 983044
  62.5 43.7 %collective-permute-start.2 = (bf16[320,512]{1,0:T(8,128)(2,1)S(1)}, bf16[320,512]{1,0:T(8,128)(2,1)S(1)}, u32[]{:S(2)}, u32[]{:S(2)}) collective-permute-start(bf16[320,512]{1,0:T(8,128)(2,1)S(1)} %get-tuple-element.15), channel_id=1, source_target_pairs={{0,2},{2,4},{4,6},{6,8},{8,10},{10,12},{12,14},{14,16},{16,18},{18... | collective-permute-start | bytes 983048 | tf_op jit(solution)/shard_map/ppermute | solution.py:16
  66.5 39.7 %collective-permute-start.3 = (bf16[320,512]{1,0:T(8,128)(2,1)S(1)}, bf16[320,512]{1,0:T(8,128)(2,1)}, u32[]{:S(2)}, u32[]{:S(2)}) collective-permute-start(bf16[320,512]{1,0:T(8,128)(2,1)S(1)} %get-tuple-element.16), channel_id=1, source_target_pairs={{2,0},{4,2},{6,4},{8,6},{10,8},{12,10},{14,12},{16,14},{18,16},{20... | collective-permute-start | bytes 983048 | tf_op jit(solution)/shard_map/ppermute | solution.py:19
  124.1 21.4 %copy-start.11 = (f32[320,512]{1,0:T(8,128)S(1)}, f32[320,512]{1,0:T(8,128)}, u32[]{:S(2)}) copy-start(f32[320,512]{1,0:T(8,128)} %fusion.15) | copy-start | bytes 1966084
  147.8 39.6 %copy-start.1 = (bf16[320,512]{1,0:T(8,128)(2,1)}, bf16[320,512]{1,0:T(8,128)(2,1)S(1)}, u32[]{:S(2)}) copy-start(bf16[320,512]{1,0:T(8,128)(2,1)S(1)} %add_convert_fusion.1) | copy-start | bytes 983044
  158.3 25.9 %copy-start.7 = (bf16[2,512,512]{2,1,0:T(8,128)(2,1)S(1)}, bf16[2,512,512]{2,1,0:T(8,128)(2,1)}, u32[]{:S(2)}) copy-start(bf16[2,512,512]{2,1,0:T(8,128)(2,1)} %all-gather.13.cloned.1.call-done) | copy-start | bytes 3145732
  185.4 7.5 %collective-permute-start.4 = (bf16[320,512]{1,0:T(8,128)(2,1)S(1)}, bf16[320,512]{1,0:T(8,128)(2,1)S(1)}, u32[]{:S(2)}, u32[]{:S(2)}) collective-permute-start(bf16[320,512]{1,0:T(8,128)(2,1)S(1)} %get-tuple-element.13), channel_id=1, source_target_pairs={{0,2},{2,4},{4,6},{6,8},{8,10},{10,12},{12,14},{14,16},{16,18},{18... | collective-permute-start | bytes 983048 | tf_op jit(solution)/shard_map/ppermute | solution.py:16
  185.4 10.3 %collective-permute-start.5 = (bf16[320,512]{1,0:T(8,128)(2,1)S(1)}, bf16[320,512]{1,0:T(8,128)(2,1)S(1)}, u32[]{:S(2)}, u32[]{:S(2)}) collective-permute-start(bf16[320,512]{1,0:T(8,128)(2,1)S(1)} %get-tuple-element.14), channel_id=1, source_target_pairs={{2,0},{4,2},{6,4},{8,6},{10,8},{12,10},{14,12},{16,14},{18,16},{20... | collective-permute-start | bytes 983048 | tf_op jit(solution)/shard_map/ppermute | solution.py:19
  (16 other events, 58.0 us)
Sparse Core Ops, SparseCore 0:
  8.9 23.3 all-gather.10
  33.8 21.1 all-gather.12
  56.5 21.8 all-gather.14
  79.8 20.4 all-gather.8
  101.7 21.1 all-gather.16
  124.2 21.1 all-gather.18
where the time goes:
time: 234 us
  blocking collectives  85.7 us (37%)
  local copies, waits for them, and re-layouts  37.5 us (16%)
  matrix products  35 us (15%)
  waiting for transfers between devices  32.1 us (14%)
  other arithmetic  16.9 us (7%)
  between operations  14.2 us (6%)
  starting transfers between devices  12.2 us (5%)
    all_gather x2, blocking collectives, per_device(): everyone = lax.all_gather(send_patch[:co_dev], 'ma', axis=0, tiled=True)  49.5 us
    all_gather x1, waiting for transfers between devices, per_device(): lax.all_gather(w_node_out, 'dev', axis=1, tiled=True)  20.1 us
    dot_general x4, matrix products, edge_messages(): jnp.einsum('nkg,gd->nkd', geom, geom_weight, precision=lax.Precision.HIGH...  17 us
    all_gather x2, blocking collectives, per_device(): send_patch = lax.all_gather(send_half, 'dev', axis=0, tiled=True)  15.6 us
    reduce_sum x1, other arithmetic, per_device(): jnp.mean(pulled, axis=1)  13.7 us
    gather x2, local copies, waits for them, and re-layouts, per_device(): padded[senders_own]  12.8 us
    gather x2, local copies, waits for them, and re-layouts, per_device(): pulled = jnp.take(padded_grid, local_map, axis=0).astype(jnp.float32)  11.8 us
    all_gather x1, blocking collectives, per_device(): latent = lax.all_gather(latent, 'dev', axis=0, tiled=True)  9.66 us
  transfers between devices with their start and end apart: 12, of which 4 were waited for; matrix products, arithmetic and copies ran while one was open for 26% of the time, Pallas kernels for 0%

commit v1 on v0

v1 whole, which is shorter than its diff:
```python
import functools

import jax
import jax.numpy as jnp
from jax import lax
from jax.experimental import pallas as pl
from jax.experimental.pallas import tpu as pltpu
from jax.sharding import PartitionSpec as P

norm_eps = 1e-05
MESH = pl.DeviceIdType.MESH
slot_w = 8


def round_up(value, step):
    return (value + step - 1) // step * step


def silu(x):
    half = 0.5 * x
    return half + half * jnp.tanh(half)


def split_two(x):
    high = x.astype(jnp.bfloat16)
    low = (x - high.astype(jnp.float32)).astype(jnp.bfloat16)
    return high, low


def wrapped(index, base, total):
    v = index - base
    v = jnp.where(v < 0, v + total, v)
    return jnp.where(v >= total, v - total, v)


def kernel(
    patches,
    geo_terms,
    grid_ref,
    mesh_ref,
    map_ref,
    fine_ref,
    cidx_ref,
    fgeo_ref,
    cgeo_ref,
    prm_ref,
    ws_ref,
    wr_ref,
    wh_ref,
    wa_ref,
    wm_ref,
    wo_ref,
    mbias_ref,
    gain_ref,
    nbias_ref,
    out_ref,
    gpad,
    cmat,
    oh,
    coh,
    spad,
    ever,
    recv,
    lat,
    hsum,
    nhid,
    wc,
    wrow,
    prm,
    loc_sem,
    gs_sem,
    gr_sem,
    ys_sem,
    yr_sem,
    fs_sem,
    fr_sem,
    ps_sem,
    hs_sem,
    hr_sem,
    cs_sem,
    cr_sem,
):
    me = lax.axis_index("ma")
    dev = lax.axis_index("dev")
    other = 1 - dev
    core = lax.rem(me, 2)
    sibling = me + 1 - 2 * core
    right = lax.rem(me + 1, patches)
    left = lax.rem(me + patches - 1, patches)
    grid_dev = grid_ref.shape[0]
    node_dev, features = mesh_ref.shape
    layers = ws_ref.shape[0]
    fine_in = fine_ref.shape[1]
    half = ws_ref.shape[2]
    gb, nb = grid_dev // 2, node_dev // 2
    span = 2 * node_dev
    co_edges = cidx_ref.shape[0]
    coarse = ever.shape[1] - cgeo_ref.shape[1]
    co_dev = coarse // patches
    coarse_in = co_edges // co_dev
    blk = 128
    nblk = node_dev // blk

    barrier = pltpu.get_barrier_semaphore()

    def greet(step, _):
        peer = lax.rem(me + step, patches)
        pl.semaphore_signal(barrier, inc=1, device_id={"ma": peer}, device_id_type=MESH)
        return 0

    lax.fori_loop(1, patches, greet, 0)
    pl.semaphore_signal(barrier, inc=1, device_id={"dev": other}, device_id_type=MESH)
    pl.semaphore_wait(barrier, patches)

    to_left = pltpu.make_async_remote_copy(
        src_ref=grid_ref.at[pl.ds(0, gb)],
        dst_ref=gpad.at[pl.ds(gb + grid_dev, gb)],
        send_sem=gs_sem.at[0],
        recv_sem=gr_sem.at[0],
        device_id={"ma": left},
        device_id_type=MESH,
    )
    to_right = pltpu.make_async_remote_copy(
        src_ref=grid_ref.at[pl.ds(grid_dev - gb, gb)],
        dst_ref=gpad.at[pl.ds(0, gb)],
        send_sem=gs_sem.at[1],
        recv_sem=gr_sem.at[1],
        device_id={"ma": right},
        device_id_type=MESH,
    )
    to_left.start()
    to_right.start()
    grid_own = pltpu.make_async_copy(grid_ref, gpad.at[pl.ds(gb, grid_dev)], loc_sem.at[layers, 0])
    grid_own.start()

    prm_out = pltpu.make_async_remote_copy(
        src_ref=prm_ref,
        dst_ref=prm.at[dev],
        send_sem=ps_sem.at[0],
        recv_sem=ps_sem.at[1],
        device_id={"dev": other},
        device_id_type=MESH,
    )
    prm_out.start()
    prm_own = pltpu.make_async_copy(prm_ref, prm.at[dev], loc_sem.at[layers, 1])
    prm_own.start()
    cols = (ws_ref, wr_ref, wh_ref, wa_ref)
    rows = (wm_ref, wo_ref)
    order = (0, 1, 4, 2, 3, 5)

    def own_part(layer, i):
        if i < 4:
            n = features // 2
            return cols[i].at[layer, pl.ds(core * n, n), :]
        n = half // 2
        return rows[i - 4].at[layer, pl.ds(core * n, n), :]

    def slot(layer, i, side, part):
        if i < 4:
            n = features // 2
            return wc.at[layer, i, side, pl.ds(part * n, n), :]
        n = half // 2
        return wrow.at[layer, i - 4, pl.ds(side * half + part * n, n), :]

    def y_copy(layer, i):
        return pltpu.make_async_remote_copy(
            src_ref=own_part(layer, i),
            dst_ref=slot(layer, i, dev, core),
            send_sem=ys_sem.at[layer, i],
            recv_sem=yr_sem.at[layer, i],
            device_id={"dev": other},
            device_id_type=MESH,
        )

    def y_wait(layer, i):
        got = slot(layer, i, other, core)
        pltpu.make_async_remote_copy(
            src_ref=got,
            dst_ref=got,
            send_sem=ys_sem.at[layer, i],
            recv_sem=yr_sem.at[layer, i],
            device_id={"dev": other},
            device_id_type=MESH,
        ).wait_recv()

    def f_copy(layer, i, part):
        got = slot(layer, i, other, part)
        return pltpu.make_async_remote_copy(
            src_ref=got,
            dst_ref=got,
            send_sem=fs_sem.at[layer, i],
            recv_sem=fr_sem.at[layer, i],
            device_id={"ma": sibling},
            device_id_type=MESH,
        )

    def local_copy(layer, i):
        if i < 4:
            return pltpu.make_async_copy(
                cols[i].at[layer], wc.at[layer, i, dev], loc_sem.at[layer, i]
            )
        return pltpu.make_async_copy(
            rows[i - 4].at[layer],
            wrow.at[layer, i - 4, pl.ds(dev * half, half), :],
            loc_sem.at[layer, i],
        )

    for layer in range(layers):
        for i in order:
            y_copy(layer, i).start()
    for layer in range(layers):
        for i in order:
            local_copy(layer, i).start()

    def forward(layer, i):
        y_wait(layer, i)
        f_copy(layer, i, core).start()

    def ready(layer, i):
        local_copy(layer, i).wait()
        f_copy(layer, i, 1 - core).wait_recv()

    ext = fgeo_ref.shape[1]
    base = me * node_dev - nb
    gbase = me * grid_dev - gb

    def counts(b, _):
        r = pl.ds(b * blk, blk)
        idx = wrapped(map_ref[r, :], gbase, grid_dev * patches)
        lanes = lax.broadcasted_iota(jnp.int32, (blk, 2 * grid_dev), 1)
        total = jnp.zeros((blk, 2 * grid_dev), jnp.float32)
        for k in range(map_ref.shape[1]):
            total = total + jnp.where(lanes == idx[:, k : k + 1], 1.0, 0.0)
        cmat[r, :] = total.astype(jnp.bfloat16)
        return 0

    lax.fori_loop(0, nblk, counts, 0)

    glane = lax.broadcasted_iota(jnp.int32, (blk, ext), 1)
    gterm = fine_in * slot_w

    def one_hots(b, _):
        r = pl.ds(b * blk, blk)
        idx = wrapped(fine_ref[r, :], base, node_dev * patches)
        lanes = lax.broadcasted_iota(jnp.int32, (blk, span), 1)
        high, low = split_two(fgeo_ref[r, :])
        both = jnp.where(glane < 2 * gterm, high.astype(jnp.float32), low.astype(jnp.float32))
        which = lax.rem(lax.div(glane, slot_w), fine_in)
        for j in range(fine_in):
            oh[j, r, :span] = jnp.where(lanes == idx[:, j : j + 1], 1.0, 0.0).astype(jnp.bfloat16)
            oh[j, r, span:] = jnp.where(which == j, both, 0.0).astype(jnp.bfloat16)
        return 0

    lax.fori_loop(0, nblk, one_hots, 0)

    clanes = lax.broadcasted_iota(jnp.int32, (co_edges, coarse), 1)
    coh[:, :coarse] = jnp.where(clanes == cidx_ref[...], 1.0, 0.0).astype(jnp.bfloat16)
    cext = cgeo_ref.shape[1]
    high, low = split_two(cgeo_ref[...])
    clane = lax.broadcasted_iota(jnp.int32, (co_edges, cext), 1)
    coh[:, coarse:] = jnp.where(
        clane < 2 * slot_w, high.astype(jnp.float32), low.astype(jnp.float32)
    ).astype(jnp.bfloat16)

    prm_own.wait()
    prm_in = pltpu.make_async_remote_copy(
        src_ref=prm.at[other],
        dst_ref=prm.at[other],
        send_sem=ps_sem.at[0],
        recv_sem=ps_sem.at[1],
        device_id={"dev": other},
        device_id_type=MESH,
    )
    prm_in.wait_recv()
    for layer in range(layers):
        for side in range(2):
            c = pl.ds(side * half, half)
            high, low = split_two(prm[side, layer])
            high, low = high.astype(jnp.float32), low.astype(jnp.float32)
            pad = ext - geo_terms * gterm
            pieces = [high] * fine_in + [low] * fine_in + [high] * fine_in
            if pad:
                pieces.append(jnp.zeros((pad, half), jnp.float32))
            spad[layer, span:, c] = jnp.concatenate(pieces, axis=0).astype(jnp.bfloat16)
            pieces = [high, low, high]
            pieces.append(jnp.zeros((cext - geo_terms * slot_w, half), jnp.float32))
            ever[layer, coarse:, c] = jnp.concatenate(pieces, axis=0).astype(jnp.bfloat16)

    for i in (0, 1):
        forward(0, i)
    grid_own.wait()
    to_left.wait_recv()
    to_right.wait_recv()

    def encode(b, _):
        r = pl.ds(b * blk, blk)
        mean = jnp.dot(cmat[r, :], gpad[...], preferred_element_type=jnp.float32)
        mean = mean * (1.0 / map_ref.shape[1])
        lat[r, :] = (mesh_ref[r, :].astype(jnp.float32) + mean).astype(jnp.bfloat16)
        return 0

    lax.fori_loop(0, nblk, encode, 0)

    for layer in range(layers):
        ready(layer, 0)

        def project_send(b, _):
            r = pl.ds(b * blk, blk)
            x = lat[r, :]
            for side in range(2):
                spad[layer, pl.ds(nb + b * blk, blk), side * half : (side + 1) * half] = jnp.dot(
                    x, wc[layer, 0, side], preferred_element_type=jnp.float32
                ).astype(jnp.bfloat16)
            return 0

        lax.fori_loop(0, nblk, project_send, 0)

        halo_left = pltpu.make_async_remote_copy(
            src_ref=spad.at[layer, pl.ds(nb, nb), :],
            dst_ref=spad.at[layer, pl.ds(nb + node_dev, nb), :],
            send_sem=hs_sem.at[layer, 0],
            recv_sem=hr_sem.at[layer, 0],
            device_id={"ma": left},
            device_id_type=MESH,
        )
        halo_right = pltpu.make_async_remote_copy(
            src_ref=spad.at[layer, pl.ds(node_dev, nb), :],
            dst_ref=spad.at[layer, pl.ds(0, nb), :],
            send_sem=hs_sem.at[layer, 1],
            recv_sem=hr_sem.at[layer, 1],
            device_id={"ma": right},
            device_id_type=MESH,
        )
        halo_left.start()
        halo_right.start()

        def coarse_copy(step):
            peer = lax.rem(me + step, patches)
            return pltpu.make_async_remote_copy(
                src_ref=spad.at[layer, pl.ds(nb, co_dev), :],
                dst_ref=ever.at[layer, pl.ds(me * co_dev, co_dev), :],
                send_sem=cs_sem.at[layer, step],
                recv_sem=cr_sem.at[layer, step],
                device_id={"ma": peer},
                device_id_type=MESH,
            )

        def coarse_start(step, _):
            coarse_copy(step).start()
            return 0

        lax.fori_loop(1, patches, coarse_start, 0)
        ever[layer, pl.ds(pl.multiple_of(me * co_dev, co_dev), co_dev), :] = spad[
            layer, nb : nb + co_dev, :
        ]

        ready(layer, 1)

        def project_recv(b, _):
            r = pl.ds(b * blk, blk)
            x = lat[r, :]
            for side in range(2):
                recv[r, side * half : (side + 1) * half] = jnp.dot(
                    x, wc[layer, 1, side], preferred_element_type=jnp.float32
                ).astype(jnp.bfloat16)
            return 0

        lax.fori_loop(0, nblk, project_recv, 0)
        for i in (4, 2, 3, 5):
            if layer == 0:
                forward(0, i)

        halo_left.wait_recv()
        halo_right.wait_recv()

        def edges(b, _):
            r = pl.ds(b * blk, blk)
            x = recv[r, :].astype(jnp.float32)
            total = jnp.zeros((blk, features), jnp.float32)
            for j in range(fine_in):
                pre = jnp.dot(oh[j, r, :], spad[layer], preferred_element_type=jnp.float32)
                total = total + silu(pre + x)
            hsum[r, :] = total
            return 0

        lax.fori_loop(0, nblk, edges, 0)

        def coarse_wait(step, _):
            source = lax.rem(me + patches - step, patches)
            got = ever.at[layer, pl.ds(source * co_dev, co_dev), :]
            pltpu.make_async_remote_copy(
                src_ref=got,
                dst_ref=got,
                send_sem=cs_sem.at[layer, step],
                recv_sem=cr_sem.at[layer, step],
                device_id={"ma": source},
                device_id_type=MESH,
            ).wait_recv()
            return 0

        lax.fori_loop(1, patches, coarse_wait, 0)
        cpre = jnp.dot(coh[...], ever[layer], preferred_element_type=jnp.float32)
        x = recv[:co_dev, :].astype(jnp.float32)
        total = hsum[:co_dev, :]
        for j in range(coarse_in):
            total = total + silu(cpre[j * co_dev : (j + 1) * co_dev, :] + x)
        hsum[:co_dev, :] = total

        if layer + 1 < layers:
            for i in order:
                forward(layer + 1, i)
        for i in (4, 2, 3, 5):
            ready(layer, i)

        def nodes(b, _):
            r = pl.ds(b * blk, blk)
            agg = jnp.dot(
                hsum[r, :].astype(jnp.bfloat16), wrow[layer, 0], preferred_element_type=jnp.float32
            )
            position = b * blk + lax.broadcasted_iota(jnp.int32, (blk, features), 0)
            count = jnp.where(position < co_dev, float(fine_in + coarse_in), float(fine_in))
            agg = (agg + count * mbias_ref[layer : layer + 1, :]).astype(jnp.bfloat16)
            x = lat[r, :]
            for side in range(2):
                pre = (
                    jnp.dot(x, wc[layer, 2, side], preferred_element_type=jnp.float32)
                    + jnp.dot(agg, wc[layer, 3, side], preferred_element_type=jnp.float32)
                    + prm[side, layer, 5:6, :]
                )
                nhid[r, side * half : (side + 1) * half] = silu(pre).astype(jnp.bfloat16)
            update = jnp.dot(nhid[r, :], wrow[layer, 1], preferred_element_type=jnp.float32)
            average = jnp.mean(update, axis=1, keepdims=True)
            spread = jnp.mean(update * update, axis=1, keepdims=True) - average * average
            normed = (update - average) * lax.rsqrt(spread + norm_eps)
            normed = normed * gain_ref[layer : layer + 1, :] + nbias_ref[layer : layer + 1, :]
            result = (x.astype(jnp.float32) + normed).astype(jnp.bfloat16)
            if layer + 1 < layers:
                lat[r, :] = result
            else:
                out_ref[r, :] = result
            return 0

        lax.fori_loop(0, nblk, nodes, 0)

        halo_left.wait_send()
        halo_right.wait_send()

        def coarse_done(step, _):
            coarse_copy(step).wait_send()
            return 0

        lax.fori_loop(1, patches, coarse_done, 0)

    to_left.wait_send()
    to_right.wait_send()
    prm_out.wait_send()
    for layer in range(layers):
        for i in order:
            y_copy(layer, i).wait_send()
            f_copy(layer, i, core).wait_send()


def per_device(
    grid_latent,
    mesh_latent,
    grid_map,
    fine_senders,
    coarse_senders,
    fine_geom,
    coarse_geom,
    w_send,
    w_recv,
    w_geom,
    edge_bias,
    w_msg,
    msg_bias,
    w_node_h,
    w_node_a,
    node_bias,
    w_node_out,
    norm_gain,
    norm_bias,
):
    patches = lax.axis_size("ma")
    node_dev, features = mesh_latent.shape
    grid_dev = grid_latent.shape[0]
    co_dev, coarse_in = coarse_senders.shape
    fine_in, geo = fine_geom.shape[1], fine_geom.shape[2]
    layers, _, half = w_send.shape
    coarse = co_dev * patches
    co_edges = co_dev * coarse_in
    terms = 3
    ext = round_up(terms * slot_w * fine_in, 256)
    cext = 128

    ones = jnp.ones((node_dev, fine_in, 1), jnp.float32)
    rest = jnp.zeros((node_dev, fine_in, slot_w - geo - 1), jnp.float32)
    block = jnp.concatenate([fine_geom, ones, rest], axis=2).reshape(node_dev, fine_in * slot_w)
    fgeo = jnp.concatenate(
        [block] * terms + [jnp.zeros((node_dev, ext - terms * slot_w * fine_in), jnp.float32)],
        axis=1,
    )
    cg = jnp.transpose(coarse_geom, (1, 0, 2)).reshape(co_edges, geo)
    block = jnp.concatenate(
        [
            cg,
            jnp.ones((co_edges, 1), jnp.float32),
            jnp.zeros((co_edges, slot_w - geo - 1), jnp.float32),
        ],
        axis=1,
    )
    cgeo = jnp.concatenate(
        [block] * terms + [jnp.zeros((co_edges, cext - terms * slot_w), jnp.float32)], axis=1
    )
    cidx = jnp.transpose(coarse_senders).reshape(co_edges, 1)
    prm = jnp.concatenate(
        [
            w_geom,
            edge_bias[:, None, :],
            node_bias[:, None, :],
            jnp.zeros((layers, slot_w - geo - 2, half), jnp.float32),
        ],
        axis=1,
    )
    vmem = pl.BlockSpec(memory_space=pltpu.VMEM)
    hbm = pl.BlockSpec(memory_space=pl.ANY)
    dma = pltpu.SemaphoreType.DMA
    bf16, f32 = jnp.bfloat16, jnp.float32
    return pl.pallas_call(
        functools.partial(kernel, patches, terms),
        out_shape=jax.ShapeDtypeStruct((node_dev, features), bf16),
        in_specs=[hbm, vmem, vmem, vmem, vmem, vmem, vmem, hbm]
        + [hbm] * 6
        + [vmem] * 3,
        out_specs=vmem,
        scratch_shapes=[
            pltpu.VMEM((2 * grid_dev, features), bf16),
            pltpu.VMEM((node_dev, 2 * grid_dev), bf16),
            pltpu.VMEM((fine_in, node_dev, 2 * node_dev + ext), bf16),
            pltpu.VMEM((co_edges, coarse + cext), bf16),
            pltpu.VMEM((layers, 2 * node_dev + ext, features), bf16),
            pltpu.VMEM((layers, coarse + cext, features), bf16),
            pltpu.VMEM((node_dev, features), bf16),
            pltpu.VMEM((node_dev, features), bf16),
            pltpu.VMEM((node_dev, features), f32),
            pltpu.VMEM((node_dev, features), bf16),
            pltpu.VMEM((layers, 4, 2, features, half), bf16),
            pltpu.VMEM((layers, 2, 2 * half, features), bf16),
            pltpu.VMEM((2, layers, slot_w, half), f32),
            dma((layers + 1, 6)),
            dma((2,)),
            dma((2,)),
            dma((layers, 6)),
            dma((layers, 6)),
            dma((layers, 6)),
            dma((layers, 6)),
            dma((2,)),
            dma((layers, 2)),
            dma((layers, 2)),
            dma((layers, patches)),
            dma((layers, patches)),
        ],
        compiler_params=pltpu.CompilerParams(
            collective_id=0, has_side_effects=True, vmem_limit_bytes=60 * 1024 * 1024
        ),
        name="processor",
    )(
        grid_latent,
        mesh_latent,
        grid_map,
        fine_senders,
        cidx,
        fgeo,
        cgeo,
        prm,
        w_send,
        w_recv,
        w_node_h,
        w_node_a,
        w_msg,
        w_node_out,
        msg_bias,
        norm_gain,
        norm_bias,
    )


def solution(mesh):
    in_specs = (
        P("ma", None),
        P("ma", None),
        P("ma", None),
        P("ma", None),
        P("ma", None),
        P("ma", None, None),
        P("ma", None, None),
        P(None, None, "dev"),
        P(None, None, "dev"),
        P(None, None, "dev"),
        P(None, "dev"),
        P(None, "dev", None),
        P(),
        P(None, None, "dev"),
        P(None, None, "dev"),
        P(None, "dev"),
        P(None, "dev", None),
        P(),
        P(),
    )
    out_specs = P("ma", None)
    return jax.shard_map(
        per_device, mesh=mesh, in_specs=in_specs, out_specs=out_specs, check_vma=False
    )
```

time: 234 us -> 86.1 us (0.37)
  blocking collectives: 85.7 us -> 0 us
  Pallas kernels: 0 us -> 74.1 us
  matrix products: 35 us -> 0 us
  waiting for transfers between devices: 32.1 us -> 0 us
  local copies, waits for them, and re-layouts: 37.5 us -> 8.86 us
  other arithmetic: 16.9 us -> 2.69 us
  between operations: 14.2 us -> 0.07 us
  starting transfers between devices: 12.2 us -> 0 us
    all_gather x8 -> x0, blocking collectives: 85.7 us -> none  [the longest x2 49.5 us: per_device(): everyone = lax.all_gather(send_patch[:co_dev], 'ma', axis=0, tiled=True)]
    pallas_call x0 -> x1, Pallas kernels: none -> 74.1 us  [per_device(): pl.pallas_call(functools.partial(kernel, patches, terms), out_shape=jax.S...]
    dot_general x16 -> x0, matrix products: 35 us -> none  [the longest x4 17 us: edge_messages(): jnp.einsum('nkg,gd->nkd', geom, geom_weight, precision=lax.Precision.HIGH...]
    gather x6 -> x0, local copies, waits for them, and re-layouts: 28.7 us -> none  [the longest x2 12.8 us: per_device(): padded[senders_own]]
    all_gather x6 -> x0, waiting for transfers between devices: 20.2 us -> none  [the longest x1 20.1 us: per_device(): lax.all_gather(w_node_out, 'dev', axis=1, tiled=True)]
    reduce_sum x1 -> x0, other arithmetic: 13.7 us -> none  [per_device(): jnp.mean(pulled, axis=1)]
    ppermute x6 -> x0, starting transfers between devices: 12 us -> none  [the longest x3 6.62 us: padded_2(): lax.ppermute(lax.slice_in_dim(block, block.shape[dim] - width, None, axis...]
    ppermute x6 -> x0, waiting for transfers between devices: 8.72 us -> none  [the longest x3 4.37 us: padded_2(): lax.ppermute(lax.slice_in_dim(block, block.shape[dim] - width, None, axis...]
  transfers between devices with their start and end apart: 12 -> 0, of which waited for: 4 -> 0; matrix products, arithmetic and copies ran while one was open for 26% -> 0% of each run, Pallas kernels for 0% -> 0%
where the time goes in v1:
time: 86.1 us; the launch traced here: 85.7 us
  Pallas kernels  74.1 us (86%)
  local copies, waits for them, and re-layouts  8.86 us (10%)
  other arithmetic  2.69 us (3%)
    pallas_call x1, Pallas kernels, per_device(): pl.pallas_call(functools.partial(kernel, patches, terms), out_shape=jax.S...  74.1 us
    unnamed x11, local copies, waits for them, and re-layouts  3.82 us

profile of v1, /device:TPU:1, one launch (start us, length us, event | category | flops | bytes accessed | tf_op | source)
XLA Modules:
  0.0 85.7 jit_solution(4407403969518344625)
XLA Ops:
  0.0 0.1 pad.9.clone
  0.1 0.1 pad.3.clone
  0.2 0.1 pad.7.clone
  0.2 0.1 pad.10.clone
  0.3 0.7 broadcast_in_dim.33
  1.0 0.7 broadcast_in_dim.34
  1.7 1.4 %maximum_maximum_fusion.1.prm_ref = f32[2,8,256]{2,1,0:T(8,128)} fusion(f32[2,1,256]{2,1,0:T(1,128)S(1)} %broadcast_in_dim.34, f32[2,1,256]{2,1,0:T(1,128)S(1)} %broadcast_in_dim.33, f32[2,4,256]{2,1,0:T(4,128)} %param.28, f32[8]{0:T(128)S(1)} %pad.3.clone), kind=kLoop, calls=%fused_computation.2 | loop fusion | flops 12288 | bytes 28704 | tf_op jit(solution)/shard_map/concatenate | solution.py:516
  3.0 0.8 copy.25
  3.8 0.0 copy-done
  3.8 0.1 maximum_bitcast_fusion
  3.9 0.0 copy-start.1
  3.9 0.8 reshape.12.cidx_ref
  4.7 0.0 copy-done.1
  4.7 0.2 copy.29
  5.0 1.4 %concatenate.16.cgeo_ref = f32[384,128]{1,0:T(8,128)} concatenate(f32[384,4]{1,0:T(8,128)S(1)} %bitcast.6, f32[384,1]{1,0:T(8,128)S(1)} %broadcast_in_dim.30, f32[384,3]{1,0:T(8,128)S(1)} %broadcast_in_dim.31, f32[384,4]{1,0:T(8,128)S(1)} %bitcast.7, f32[384,1]{1,0:T(8,128)S(1)} %broadcast_in_dim.30, f32[384,3]{1,0:T(8,128)S(1)} %broadcast_in_dim.31, f32[384,4]{1,0:T(8,128)S(1)} %bitcast.8, ...), dimensions={1} | concatenate | bytes 393216 | tf_op jit(solution)/shard_map/concatenate | solution.py:512
  6.4 0.2 copy.26
  6.5 0.0 copy-start.3
  6.6 1.2 %maximum_maximum_fusion.fgeo_ref = f32[640,256]{1,0:T(8,128)} fusion(f32[640,48]{1,0:T(8,128)S(1)} %copy.26, f32[256]{0:T(256)S(1)} %pad.7.clone), kind=kLoop, calls=%fused_computation | loop fusion | flops 491520 | bytes 779264 | tf_op jit(solution)/shard_map/concatenate | solution.py:499
  7.8 0.0 copy-done.3
  7.8 0.9 %copy.30.map_ref = s32[640,4]{1,0:T(8,128)} copy(s32[640,4]{0,1:T(4,128)S(1)} %copy-done.3) | data formatting | bytes 20480 | tf_op args[2]
  8.7 0.0 copy-done.2
  8.7 0.9 %copy.31.fine_ref = s32[640,6]{1,0:T(8,128)} copy(s32[640,6]{0,1:T(8,128)S(1)} %copy-done.2) | data formatting | bytes 30720 | tf_op args[3]
  9.7 74.1 %processor.1 = bf16[640,512]{1,0:T(8,128)(2,1)} custom-call(bf16[1024,512]{1,0:T(8,128)(2,1)} %grid_ref.1, bf16[640,512]{1,0:T(8,128)(2,1)} %mesh_ref.1, s32[640,4]{1,0:T(8,128)} %copy.30.map_ref, s32[640,6]{1,0:T(8,128)} %copy.31.fine_ref, s32[384,1]{1,0:T(8,128)} %reshape.12.cidx_ref, f32[640,256]{1,0:T(8,128)} %maximum_maximum_fusion.fgeo_ref, ...), custom_call_target="tpu_custom_call" | custom-call | tf_op jit(solution)/shard_map/processor/pallas_call | solution.py:529
  83.8 2.0 %copy.34 = bf16[640,512]{1,0:T(8,128)(2,1)} copy(bf16[640,512]{1,0:T(8,128)(2,1)} %processor.1) | data formatting | bytes 1310720
  (8 shorter events, 0.1 us)
Async XLA Ops:
  0.0 3.8 %copy-start = (f32[640,6,4]{0,2,1:T(4,128)S(1)}, f32[640,6,4]{0,2,1:T(4,128)}, u32[]{:S(2)}) copy-start(f32[640,6,4]{0,2,1:T(4,128)} %param.24) | copy-start | bytes 184324
  3.9 0.8 copy-start.1
  6.5 1.3 %copy-start.3 = (s32[640,4]{0,1:T(4,128)S(1)}, s32[640,4]{0,1:T(4,128)}, u32[]{:S(2)}) copy-start(s32[640,4]{0,1:T(4,128)} %param.21) | copy-start | bytes 30724
  7.8 0.9 %copy-start.2 = (s32[640,6]{0,1:T(8,128)S(1)}, s32[640,6]{0,1:T(8,128)}, u32[]{:S(2)}) copy-start(s32[640,6]{0,1:T(8,128)} %param.22) | copy-start | bytes 46084
